TPU v7x, 256 devices: a whole 4x4x8 slice. The times are simulated.
256 devices in a mesh: seg: 4 (over z_hi), ch: 64 (over x, y, z_lo, core).
Axes of the slice: x: 4, y: 4, z: 8 (z_hi: 4, z_lo: 2; z = z_hi * 2 + z_lo), core: 2. Of those that a mesh axis runs over, the one named last changes fastest.
Arguments:
- gate_in: bfloat16 [1536, 16384], P('ch', 'seg'), may hold values from -6 to 6
- key_in: bfloat16 [1536, 16384], P('ch', 'seg'), may hold values from -6 to 6
- value_in: bfloat16 [1536, 16384], P('ch', 'seg'), may hold values from -6 to 6
- kernel: float32 [1536, 16384], P('ch'), may hold values from -0.046875 to 0.046875
- skip_gain: float32 [1536], P('ch'), may hold values from -1 to 1
- out_weight: bfloat16 [1536, 1536], P('ch'), may hold values from -0.15625 to 0.15625
Outputs:
- output: bfloat16 [16384, 1536], P(('seg', 'ch'))
All inputs are finite; a program needn't handle non-finite values.
Results may differ from a plain program's by a relative error of at most 0.0095.
Values may be sent and summed in bfloat16 or wider, within the bound.
A program may use at most 64 MiB of HBM per device.

v0:
```python
import math
import jax
import jax.numpy as jnp
from jax import lax
from jax.sharding import Mesh
from jax.sharding import PartitionSpec as P

CH = ("ch_0", "ch_1", "ch_2", "ch_3")
SEG_CH = ("seg", "ch_0", "ch_1", "ch_2", "ch_3")
lane_width = 128
highest = lax.Precision.HIGHEST


def in_blocks(x, dim, devices):
    lengths = x.shape
    parts = x.reshape(*lengths[:dim], devices, lengths[dim] // devices, *lengths[dim + 1 :])
    return jnp.moveaxis(parts, dim, 0)


def in_order(parts, dim):
    lengths = list(parts.shape[1:])
    lengths[dim] *= parts.shape[0]
    return jnp.moveaxis(parts, 0, dim).reshape(lengths)


def turned_blocks(parts, axes, order):
    lengths = [lax.axis_size(a) for a in axes]
    parts = parts.reshape(*lengths, *parts.shape[1:])
    for k in order:
        parts = lax.all_to_all(parts, axes[k], split_axis=k, concat_axis=k, tiled=True)
    return parts.reshape(-1, *parts.shape[len(axes) :])


def core_and_chips(x, groups, order, split_dim, concat_dim):
    devices = lax.axis_size(groups[0]) * lax.axis_size(groups[1])
    parts = in_blocks(x, split_dim, devices)
    return in_order(turned_blocks(parts, groups, order), concat_dim)


def angle_pair(height, breadth, period):
    product = (
        jnp.arange(height, dtype=jnp.int32)[:, None]
        * jnp.arange(breadth, dtype=jnp.int32)[None, :]
        % period
    )
    theta = product.astype(jnp.float32) * (2.0 * math.pi / period)
    return (jnp.cos(theta), jnp.sin(theta))


def make_tables(outer):
    cos_outer, sin_outer = angle_pair(outer, outer, outer)
    cos_inner, sin_inner = angle_pair(lane_width, lane_width, lane_width)
    cos_twist, sin_twist = angle_pair(outer, lane_width, outer * lane_width)
    return (cos_outer, sin_outer, cos_inner, sin_inner, cos_twist, sin_twist)


def left_mul(matrix, stack):
    return jnp.einsum("kn,cnm->ckm", matrix, stack, precision=highest)


def right_mul(stack, matrix):
    return jnp.einsum("ckn,nm->ckm", stack, matrix, precision=highest)


def forward(signal, tables):
    cos_outer, sin_outer, cos_inner, sin_inner, cos_twist, sin_twist = tables
    height = signal.shape[1]
    real_a = left_mul(cos_outer[:, :height], signal)
    imag_a = -left_mul(sin_outer[:, :height], signal)
    real_b = real_a * cos_twist + imag_a * sin_twist
    imag_b = imag_a * cos_twist - real_a * sin_twist
    real_x = right_mul(real_b, cos_inner) + right_mul(imag_b, sin_inner)
    imag_x = right_mul(imag_b, cos_inner) - right_mul(real_b, sin_inner)
    return (real_x, imag_x)


def inverse_upper(real_x, imag_x, tables):
    cos_outer, sin_outer, cos_inner, sin_inner, cos_twist, sin_twist = tables
    real_c = right_mul(real_x, cos_inner) - right_mul(imag_x, sin_inner)
    imag_c = right_mul(imag_x, cos_inner) + right_mul(real_x, sin_inner)
    real_d = real_c * cos_twist - imag_c * sin_twist
    imag_d = imag_c * cos_twist + real_c * sin_twist
    middle = cos_outer.shape[0] // 2
    signal = left_mul(cos_outer[middle:], real_d) - left_mul(sin_outer[middle:], imag_d)
    return signal / float(cos_outer.shape[0] * lane_width)


def on_device(gate_in, key_in, value_in, kernel, skip_gain, out_weight):
    seg_index = lax.axis_index("seg")
    col_gate, col_key, col_value = (
        lax.all_to_all(gate_in, "seg", split_axis=0, concat_axis=1, tiled=True),
        lax.all_to_all(key_in, "seg", split_axis=0, concat_axis=1, tiled=True),
        lax.all_to_all(value_in, "seg", split_axis=0, concat_axis=1, tiled=True),
    )
    col_count, full_len = col_key.shape
    long_outer = 2 * full_len // lane_width
    long_tables = make_tables(long_outer)
    first = seg_index * col_count
    my_kernel = lax.dynamic_slice_in_dim(kernel, first, col_count, 0)
    my_skip = lax.dynamic_slice_in_dim(skip_gain, first, col_count, 0)
    col_mixed = col_key.astype(jnp.float32) * col_value.astype(jnp.float32)
    long_filter = jnp.concatenate(
        [jnp.zeros((col_count, full_len), jnp.float32), my_kernel], axis=1
    )
    filt_re, filt_im = forward(long_filter.reshape(col_count, long_outer, lane_width), long_tables)
    sig_re, sig_im = forward(col_mixed.reshape(col_count, long_outer // 2, lane_width), long_tables)
    prod_re = filt_re * sig_re - filt_im * sig_im
    prod_im = filt_re * sig_im + filt_im * sig_re
    col_conv = inverse_upper(prod_re, prod_im, long_tables).reshape(col_count, full_len)
    col_gated = (col_gate.astype(jnp.float32) * (col_conv + my_skip[:, None] * col_mixed)).astype(
        jnp.bfloat16
    )
    gated = lax.all_to_all(col_gated, "seg", split_axis=1, concat_axis=0, tiled=True)
    local_tokens = core_and_chips(gated, (("ch_0", "ch_1", "ch_2"), "ch_3"), (1, 0), 1, 0)
    result = lax.dot_general(
        local_tokens,
        lax.all_gather(out_weight, CH, axis=0, tiled=True),
        (((0,), (0,)), ((), ())),
        preferred_element_type=jnp.float32,
    )
    return result.astype(jnp.bfloat16)


def solution(mesh):
    torus = Mesh(
        mesh.devices.reshape(mesh.shape["seg"], 4, 4, 2, 2), ("seg", "ch_0", "ch_1", "ch_2", "ch_3")
    )
    in_specs = (P(CH, "seg"), P(CH, "seg"), P(CH, "seg"), P(CH, None), P(CH), P(CH, None))
    out_specs = P(SEG_CH, None)
    return jax.shard_map(
        on_device, mesh=torus, in_specs=in_specs, out_specs=out_specs, check_vma=False
    )
```

profile of v0, /device:TPU:1, one launch (start us, length us, event | category | flops | bytes accessed | tf_op | source)
XLA Modules:
  0.0 142.8 jit_solution(324831738904473637)
XLA Ops:
  6.5 1.8 %all_to_all.48 = bf16[4,6,4096]{2,1,0:T(8,128)(2,1)} reshape(bf16[24,4096]{1,0:T(8,128)(2,1)} %param.7) | data formatting | bytes 393216 | tf_op jit(solution)/shard_map/all_to_all | solution.py:92
  8.3 9.0 %all-to-all-start.1 = ((bf16[4,6,4096]{2,1,0:T(8,128)(2,1)}), bf16[4,6,4096]{2,1,0:T(8,128)(2,1)}, u32[]{:S(2)}, u32[]{:S(2)}) async-start(bf16[4,6,4096]{2,1,0:T(8,128)(2,1)} %all_to_all.48), calls=%async_computation.1 | async-start | bytes 524288 | tf_op jit(solution)/shard_map/all_to_all | solution.py:92
  18.6 1.7 %fusion.36 = f32[256,256]{1,0:T(8,128)} fusion(), kind=kLoop, calls=%fused_computation.67 | loop fusion | flops 917504 | bytes 262144 | tf_op jit(solution)/shard_map/cos | solution.py:47
  20.3 1.7 %all_to_all.50 = bf16[4,6,4096]{2,1,0:T(8,128)(2,1)} reshape(bf16[24,4096]{1,0:T(8,128)(2,1)} %param.8) | data formatting | bytes 393216 | tf_op jit(solution)/shard_map/all_to_all | solution.py:93
  22.1 2.3 %convolution_bitcast_fusion = f32[6,256,128]{1,2,0:T(8,128)S(1)} fusion(f32[1,6,256,128]{3,1,2,0:T(8,128)S(1)} %pad_bitcast_fusion), kind=kOutput, calls=%fused_computation.9 | convolution fusion | flops 604897280 | bytes 1572864 | tf_op jit(solution)/shard_map/kn,cnm->ckm/dot_general | solution.py:58
  24.4 2.3 %fusion = f32[6,256,128]{1,2,0:T(8,128)S(1)} fusion(f32[1,6,256,128]{3,1,2,0:T(8,128)S(1)} %pad_bitcast_fusion), kind=kOutput, calls=%fused_computation.8 | convolution fusion | flops 605093888 | bytes 1572864 | tf_op jit(solution)/shard_map/kn,cnm->ckm/dot_general | solution.py:58
  28.4 2.5 %convolution_add_fusion.2 = f32[6,256,128]{2,1,0:T(8,128)} fusion(f32[6,256,128]{2,1,0:T(8,128)S(1)} %fusion.38, f32[6,256,128]{1,2,0:T(8,128)S(1)} %convolution_bitcast_fusion, f32[6,256,128]{1,2,0:T(8,128)S(1)} %fusion, f32[256,128]{0,1:T(8,128)S(1)} %get-tuple-element.7, f32[256,128]{0,1:T(8,128)S(1)} %get-tuple-element.8), kind=kOutput, calls=%fused_computation.6 | convolution fusion | flops 303005696 | bytes 3407872 | tf_op jit(solution)/shard_map/ckn,nm->ckm/dot_general | solution.py:62
  30.9 6.6 %all-to-all-start.2 = ((bf16[4,6,4096]{2,1,0:T(8,128)(2,1)}), bf16[4,6,4096]{2,1,0:T(8,128)(2,1)}, u32[]{:S(2)}, u32[]{:S(2)}) async-start(bf16[4,6,4096]{2,1,0:T(8,128)(2,1)} %all_to_all.50), calls=%async_computation.2 | async-start | bytes 524288 | tf_op jit(solution)/shard_map/all_to_all | solution.py:93
  37.5 1.7 %fusion.35 = f32[256,256]{1,0:T(8,128)} fusion(), kind=kLoop, calls=%fused_computation.66 | loop fusion | flops 917504 | bytes 262144 | tf_op jit(solution)/shard_map/sin | solution.py:47
  39.3 1.7 %all_to_all.46 = bf16[4,6,4096]{2,1,0:T(8,128)(2,1)} reshape(bf16[24,4096]{1,0:T(8,128)(2,1)} %param.6) | data formatting | bytes 393216 | tf_op jit(solution)/shard_map/all_to_all | solution.py:91
  41.0 2.5 %fusion.39 = f32[6,256,128]{2,1,0:T(8,128)} fusion(f32[6,256,128]{1,2,0:T(8,128)S(1)} %convolution_bitcast_fusion, f32[6,256,128]{1,2,0:T(8,128)S(1)} %fusion, f32[256,128]{0,1:T(8,128)S(1)} %get-tuple-element.7, f32[256,128]{0,1:T(8,128)S(1)} %get-tuple-element.8), kind=kOutput, calls=%fused_computation.70 | convolution fusion | flops 302809088 | bytes 2621440 | tf_op jit(solution)/shard_map/ckn,nm->ckm/dot_general | solution.py:62
  43.5 5.5 %all-to-all-done.2 = bf16[4,6,4096]{2,1,0:T(8,128)(2,1)} async-done(((bf16[4,6,4096]{2,1,0:T(8,128)(2,1)}), bf16[4,6,4096]{2,1,0:T(8,128)(2,1)}, u32[]{:S(2)}, u32[]{:S(2)}) %all-to-all-start.2) | async-done | bytes 196640 | tf_op jit(solution)/shard_map/all_to_all | solution.py:93
  49.0 4.0 %all-to-all-start = ((bf16[4,6,4096]{2,1,0:T(8,128)(2,1)}), bf16[4,6,4096]{2,1,0:T(8,128)(2,1)}, u32[]{:S(2)}, u32[]{:S(2)}) async-start(bf16[4,6,4096]{2,1,0:T(8,128)(2,1)} %all_to_all.46), calls=%async_computation | async-start | bytes 524288 | tf_op jit(solution)/shard_map/all_to_all | solution.py:91
  55.2 2.0 %mul.450 = f32[6,128,128]{2,1,0:T(8,128)} reshape(f32[6,4,4096]{2,1,0:T(4,128)} %copy.64) | data formatting | bytes 786432 | tf_op jit(solution)/shard_map/mul | solution.py:101
  57.2 1.8 %convolution_bitcast_fusion.1 = f32[6,256,128]{1,2,0:T(8,128)S(1)} fusion(f32[6,128,128]{2,1,0:T(8,128)} %mul.450, f32[256,256]{1,0:T(8,128)} %fusion.36), kind=kOutput, calls=%fused_computation.12 | convolution fusion | flops 301989888 | bytes 1310720 | tf_op jit(solution)/shard_map/kn,cnm->ckm/dot_general | solution.py:58
  59.0 1.8 %fusion.1 = f32[6,256,128]{1,2,0:T(8,128)S(1)} fusion(f32[6,128,128]{2,1,0:T(8,128)} %mul.450, f32[256,256]{1,0:T(8,128)} %fusion.35), kind=kOutput, calls=%fused_computation.11 | convolution fusion | flops 302186496 | bytes 1310720 | tf_op jit(solution)/shard_map/kn,cnm->ckm/dot_general | solution.py:58
  64.1 1.6 %convolution_add_fusion.1 = f32[6,256,128]{2,1,0:T(8,128)S(1)} fusion(f32[6,256,128]{2,1,0:T(8,128)S(1)} %fusion.40, f32[6,256,128]{1,2,0:T(8,128)S(1)} %convolution_bitcast_fusion.1, f32[6,256,128]{1,2,0:T(8,128)S(1)} %fusion.1, f32[256,128]{0,1:T(8,128)S(1)} %get-tuple-element.7, f32[256,128]{0,1:T(8,128)S(1)} %get-tuple-element.8), kind=kOutput, calls=%fused_computation.5 | convolution fusion | flops 303005696 | bytes 3407872 | tf_op jit(solution)/shard_map/ckn,nm->ckm/dot_general | solution.py:62
  65.8 1.6 %convolution_subtract_fusion.1 = f32[6,256,128]{2,1,0:T(8,128)S(1)} fusion(f32[6,256,128]{2,1,0:T(8,128)S(1)} %fusion.41, f32[6,256,128]{1,2,0:T(8,128)S(1)} %fusion.1, f32[6,256,128]{1,2,0:T(8,128)S(1)} %convolution_bitcast_fusion.1, f32[256,128]{0,1:T(8,128)S(1)} %get-tuple-element.7, f32[256,128]{0,1:T(8,128)S(1)} %get-tuple-element.8), kind=kOutput, calls=%fused_computation.3 | convolution fusion | flops 303005696 | bytes 3407872 | tf_op jit(solution)/shard_map/ckn,nm->ckm/dot_general | solution.py:62
  67.4 1.7 %multiply_subtract_fusion = (f32[6,256,128]{2,1,0:T(8,128)S(1)}, f32[6,256,128]{2,1,0:T(8,128)S(1)}) fusion(f32[6,256,128]{2,1,0:T(8,128)S(1)} %convolution_subtract_fusion.1, f32[6,256,128]{2,1,0:T(8,128)S(1)} %copy-done.2, f32[6,256,128]{2,1,0:T(8,128)S(1)} %convolution_add_fusion.1, f32[6,256,128]{2,1,0:T(8,128)S(1)} %copy-done.1, ...), kind=kOutput, calls=%fused_computation.27 | convolution fusion | flops 304185344 | bytes 6553600 | tf_op jit(solution)/shard_map/ckn,nm->ckm/dot_general | solution.py:62
  77.2 15.5 %all_to_all.62 = bf16[6,4,4096]{2,0,1:T(8,128)(2,1)S(1)} all-to-all(bf16[6,4,4096]{2,0,1:T(8,128)(2,1)S(1)} %fusion.16), channel_id=1, replica_groups=mesh['seg'=4,'ch_0'=4,'ch_1'=4,'ch_2'=2,'ch_3'=2] {'seg'}, dimensions={1} | all-to-all | bytes 393216 | tf_op jit(solution)/shard_map/all_to_all | solution.py:113
  93.6 9.4 %all_to_all.63 = bf16[2,2,24576]{2,1,0:T(2,128)(2,1)S(1)} all-to-all(bf16[2,2,24576]{2,1,0:T(2,128)(2,1)S(1)} %reshape.86), channel_id=1, replica_groups=mesh['seg'=4,'ch_0'=4,'ch_1'=4,'ch_2'=2,'ch_3'=2] {'ch_3'}, dimensions={0} | all-to-all | bytes 393216 | tf_op jit(solution)/shard_map/all_to_all | solution.py:30
  103.6 11.6 %all_to_all.64 = bf16[32,2,1536]{2,1,0:T(2,128)(2,1)S(1)} all-to-all(bf16[32,2,1536]{2,1,0:T(2,128)(2,1)S(1)} %reshape.88), channel_id=1, replica_groups=mesh['seg'=4,'ch_0'=4,'ch_1'=4,'ch_2'=2,'ch_3'=2] {'ch_0','ch_1','ch_2'}, dimensions={0} | all-to-all | bytes 393216 | tf_op jit(solution)/shard_map/all_to_all | solution.py:30
  115.4 16.6 %all-gather.2.cloned.1.call-done = bf16[1536,1536]{1,0:T(8,128)(2,1)} async-done(((bf16[24,1536]{1,0:T(8,128)(2,1)}), bf16[1536,1536]{1,0:T(8,128)(2,1)}) %all-gather.2.cloned.1.call-update) | async-done | bytes 4718608 | tf_op jit(solution)/shard_map/all_gather | solution.py:117
  132.0 4.0 %convolution_convert_fusion = bf16[64,1536]{1,0:T(8,128)(2,1)} fusion(bf16[1536,64]{1,0:T(8,128)(2,1)S(1)} %bitcast.93, bf16[1536,1536]{1,0:T(8,128)(2,1)} %all-gather.2.cloned.1.call-done), kind=kOutput, calls=%fused_computation | convolution fusion | flops 302088192 | bytes 5111808 | tf_op jit(solution)/shard_map/dot_general | solution.py:115
  (41 shorter events, 18.2 us)
Async XLA Ops:
  6.5 15.4 %copy-start = (f32[24,16384]{1,0:T(8,128)S(1)}, f32[24,16384]{1,0:T(8,128)}, u32[]{:S(2)}) copy-start(f32[24,16384]{1,0:T(8,128)} %param.9) | copy-start | bytes 4718596
  8.3 22.5 %all-to-all-start.1 = ((bf16[4,6,4096]{2,1,0:T(8,128)(2,1)}), bf16[4,6,4096]{2,1,0:T(8,128)(2,1)}, u32[]{:S(2)}, u32[]{:S(2)}) async-start(bf16[4,6,4096]{2,1,0:T(8,128)(2,1)} %all_to_all.48), calls=%async_computation.1 | async-start | bytes 524288 | tf_op jit(solution)/shard_map/all_to_all | solution.py:92
  17.3 114.7 %all-gather.2.cloned.1.call-start = ((), (), s32[]{:S(2)}) async-start(), calls=%async_computation.6 | async-start | bytes 4792320 | tf_op jit(solution)/shard_map/all_gather | solution.py:117
  22.1 17.1 %copy-start.5 = (f32[24]{0:T(128)S(1)}, f32[24]{0:T(128)}, u32[]{:S(2)}) copy-start(f32[24]{0:T(128)} %param.10) | copy-start | bytes 292
  30.9 18.1 %all-to-all-start.2 = ((bf16[4,6,4096]{2,1,0:T(8,128)(2,1)}), bf16[4,6,4096]{2,1,0:T(8,128)(2,1)}, u32[]{:S(2)}, u32[]{:S(2)}) async-start(bf16[4,6,4096]{2,1,0:T(8,128)(2,1)} %all_to_all.50), calls=%async_computation.2 | async-start | bytes 524288 | tf_op jit(solution)/shard_map/all_to_all | solution.py:93
  49.0 26.7 %all-to-all-start = ((bf16[4,6,4096]{2,1,0:T(8,128)(2,1)}), bf16[4,6,4096]{2,1,0:T(8,128)(2,1)}, u32[]{:S(2)}, u32[]{:S(2)}) async-start(bf16[4,6,4096]{2,1,0:T(8,128)(2,1)} %all_to_all.46), calls=%async_computation | async-start | bytes 524288 | tf_op jit(solution)/shard_map/all_to_all | solution.py:91
  62.5 4.9 %copy-start.1 = (f32[6,256,128]{2,1,0:T(8,128)S(1)}, f32[6,256,128]{2,1,0:T(8,128)}, u32[]{:S(2)}) copy-start(f32[6,256,128]{2,1,0:T(8,128)} %fusion.39) | copy-start | bytes 2359300
  62.5 4.9 %copy-start.2 = (f32[6,256,128]{2,1,0:T(8,128)S(1)}, f32[6,256,128]{2,1,0:T(8,128)}, u32[]{:S(2)}) copy-start(f32[6,256,128]{2,1,0:T(8,128)} %convolution_add_fusion.2) | copy-start | bytes 2359300
  69.1 4.7 %copy-start.3 = (f32[256,256]{1,0:T(8,128)S(1)}, f32[256,256]{1,0:T(8,128)}, u32[]{:S(2)}) copy-start(f32[256,256]{1,0:T(8,128)} %fusion.36) | copy-start | bytes 786436
  70.2 4.4 %copy-start.4 = (f32[256,256]{1,0:T(8,128)S(1)}, f32[256,256]{1,0:T(8,128)}, u32[]{:S(2)}) copy-start(f32[256,256]{1,0:T(8,128)} %fusion.35) | copy-start | bytes 786436
Sparse Core Ops, SparseCore 0:
  20.0 111.9 all-gather.1
where the time goes:
time: 144 us; the launch traced here: 143 us
  blocking collectives  36.4 us (25%)
  matrix products  33.2 us (23%)
  waiting for transfers between devices  22.8 us (16%)
  starting transfers between devices  19.7 us (14%)
  between operations  13.7 us (10%)
  local copies, waits for them, and re-layouts  10.6 us (7%)
  other arithmetic  6.45 us (4%)
    all_to_all x2, blocking collectives, turned_blocks(): lax.all_to_all(parts, axes[k], split_axis=k, concat_axis=k, tiled=True)  20.9 us
    dot_general x12, matrix products, right_mul(): return jnp.einsum('ckn,nm->ckm', stack, matrix, precision=highest)  19.4 us
    all_gather x1, waiting for transfers between devices, on_device(): lax.all_gather(out_weight, CH, axis=0, tiled=True)  16.6 us
    all_to_all x1, blocking collectives, on_device(): lax.all_to_all(col_gated, 'seg', split_axis=1, concat_axis=0, tiled=True)  15.5 us
    dot_general x6, matrix products, left_mul(): return jnp.einsum('kn,cnm->ckm', matrix, stack, precision=highest)  9.87 us
    all_to_all x1, starting transfers between devices, on_device(): lax.all_to_all(key_in, 'seg', split_axis=0, concat_axis=1, tiled=True)  9 us
    all_to_all x1, starting transfers between devices, on_device(): lax.all_to_all(value_in, 'seg', split_axis=0, concat_axis=1, tiled=True)  6.64 us
    all_to_all x1, waiting for transfers between devices, on_device(): lax.all_to_all(value_in, 'seg', split_axis=0, concat_axis=1, tiled=True)  5.48 us
  transfers between devices with their start and end apart: 4, of which 2 were waited for; matrix products, arithmetic and copies ran while one was open for 29% of the time, Pallas kernels for 0%

commit v1 on v0

--- a/solution.py
+++ b/solution.py
@@ -114,7 +114,9 @@
     local_tokens = core_and_chips(gated, (("ch_0", "ch_1", "ch_2"), "ch_3"), (1, 0), 1, 0)
     result = lax.dot_general(
         local_tokens,
-        lax.all_gather(out_weight, CH, axis=0, tiled=True),
+        jnp.concatenate(
+            lax.all_to_all(jnp.stack([out_weight] * lax.axis_size(CH)), CH, 0, 0), axis=0
+        ),
         (((0,), (0,)), ((), ())),
         preferred_element_type=jnp.float32,
     )

time: 144 us -> 183 us (1.27)
  waiting for transfers between devices: 22.8 us -> 61.4 us
  between operations: 13.7 us -> 0.33 us
  starting transfers between devices: 19.7 us -> 26.6 us
  blocking collectives: 36.4 us -> 39.3 us
  local copies, waits for them, and re-layouts: 10.6 us -> 13.1 us
    all_to_all x0 -> x1, waiting for transfers between devices: none -> 59.1 us  [on_device(): lax.all_to_all(jnp.stack([out_weight] * lax.axis_size(CH)), CH, 0, 0)]
    all_gather x1 -> x0, waiting for transfers between devices: 16.6 us -> none  [on_device(): lax.all_gather(out_weight, CH, axis=0, tiled=True)]
    all_to_all x0 -> x1, starting transfers between devices: none -> 6.55 us  [on_device(): lax.all_to_all(jnp.stack([out_weight] * lax.axis_size(CH)), CH, 0, 0)]
    all_to_all x2, blocking collectives: 20.9 us -> 24.4 us  [turned_blocks(): lax.all_to_all(parts, axes[k], split_axis=k, concat_axis=k, tiled=True)]
    all_to_all x1, waiting for transfers between devices: 5.48 us -> 2.28 us  [on_device(): lax.all_to_all(value_in, 'seg', split_axis=0, concat_axis=1, tiled=True)]
    another operation x0 -> x1, local copies, waits for them, and re-layouts: none -> 2.48 us  [on_device(): jnp.stack([out_weight] * lax.axis_size(CH))]
  transfers between devices with their start and end apart: 4 -> 4, of which waited for: 2 -> 2; matrix products, arithmetic and copies ran while one was open for 29% -> 21% of each run, Pallas kernels for 0% -> 0%
where the time goes in v1:
time: 183 us; the launch traced here: 180 us
  waiting for transfers between devices  61.4 us (34%)
  blocking collectives  39.3 us (21%)
  matrix products  33.2 us (18%)
  starting transfers between devices  26.6 us (15%)
  local copies, waits for them, and re-layouts  13.1 us (7%)
  other arithmetic  6.4 us (3%)
    all_to_all x1, waiting for transfers between devices, on_device(): lax.all_to_all(jnp.stack([out_weight] * lax.axis_size(CH)), CH, 0, 0)  59.1 us
    all_to_all x2, blocking collectives, turned_blocks(): lax.all_to_all(parts, axes[k], split_axis=k, concat_axis=k, tiled=True)  24.4 us
    dot_general x12, matrix products, right_mul(): return jnp.einsum('ckn,nm->ckm', stack, matrix, precision=highest)  19.4 us
    all_to_all x1, blocking collectives, on_device(): lax.all_to_all(col_gated, 'seg', split_axis=1, concat_axis=0, tiled=True)  14.9 us
    dot_general x6, matrix products, left_mul(): return jnp.einsum('kn,cnm->ckm', matrix, stack, precision=highest)  9.87 us
    all_to_all x1, starting transfers between devices, on_device(): lax.all_to_all(key_in, 'seg', split_axis=0, concat_axis=1, tiled=True)  9 us
    all_to_all x1, starting transfers between devices, on_device(): lax.all_to_all(value_in, 'seg', split_axis=0, concat_axis=1, tiled=True)  6.64 us
    all_to_all x1, starting transfers between devices, on_device(): lax.all_to_all(jnp.stack([out_weight] * lax.axis_size(CH)), CH, 0, 0)  6.55 us
  transfers between devices with their start and end apart: 4, of which 2 were waited for; matrix products, arithmetic and copies ran while one was open for 21% of the time, Pallas kernels for 0%

profile of v1, /device:TPU:1, one launch (start us, length us, event | category | flops | bytes accessed | tf_op | source)
XLA Modules:
  0.0 180.4 jit_solution(18218738017492718728)
XLA Ops:
  0.0 1.8 %all_to_all.51 = bf16[4,6,4096]{2,1,0:T(8,128)(2,1)} reshape(bf16[24,4096]{1,0:T(8,128)(2,1)} %param.7) | data formatting | bytes 393216 | tf_op jit(solution)/shard_map/all_to_all | solution.py:92
  1.8 9.0 %all-to-all-start.1 = ((bf16[4,6,4096]{2,1,0:T(8,128)(2,1)}), bf16[4,6,4096]{2,1,0:T(8,128)(2,1)}, u32[]{:S(2)}, u32[]{:S(2)}) async-start(bf16[4,6,4096]{2,1,0:T(8,128)(2,1)} %all_to_all.51), calls=%async_computation.1 | async-start | bytes 524288 | tf_op jit(solution)/shard_map/all_to_all | solution.py:92
  10.8 1.7 fusion.36
  13.2 2.3 %fusion = f32[6,256,128]{1,2,0:T(8,128)S(1)} fusion(f32[1,6,256,128]{3,1,2,0:T(8,128)S(1)} %pad_bitcast_fusion), kind=kOutput, calls=%fused_computation.8 | convolution fusion | flops 605093888 | bytes 1572864 | tf_op jit(solution)/shard_map/kn,cnm->ckm/dot_general | solution.py:58
  15.6 2.3 %convolution_bitcast_fusion = f32[6,256,128]{1,2,0:T(8,128)S(1)} fusion(f32[1,6,256,128]{3,1,2,0:T(8,128)S(1)} %pad_bitcast_fusion), kind=kOutput, calls=%fused_computation.9 | convolution fusion | flops 604897280 | bytes 1572864 | tf_op jit(solution)/shard_map/kn,cnm->ckm/dot_general | solution.py:58
  17.8 1.7 all_to_all.53
  21.2 2.5 %convolution_add_fusion.2 = f32[6,256,128]{2,1,0:T(8,128)} fusion(f32[6,256,128]{2,1,0:T(8,128)S(1)} %fusion.38, f32[6,256,128]{1,2,0:T(8,128)S(1)} %convolution_bitcast_fusion, f32[6,256,128]{1,2,0:T(8,128)S(1)} %fusion, f32[256,128]{0,1:T(8,128)S(1)} %get-tuple-element.7, f32[256,128]{0,1:T(8,128)S(1)} %get-tuple-element.8), kind=kOutput, calls=%fused_computation.6 | convolution fusion | flops 303005696 | bytes 3407872 | tf_op jit(solution)/shard_map/ckn,nm->ckm/dot_general | solution.py:62
  23.7 6.6 %all-to-all-start.2 = ((bf16[4,6,4096]{2,1,0:T(8,128)(2,1)}), bf16[4,6,4096]{2,1,0:T(8,128)(2,1)}, u32[]{:S(2)}, u32[]{:S(2)}) async-start(bf16[4,6,4096]{2,1,0:T(8,128)(2,1)} %all_to_all.53), calls=%async_computation.2 | async-start | bytes 524288 | tf_op jit(solution)/shard_map/all_to_all | solution.py:93
  30.3 1.7 fusion.35
  32.1 1.7 all_to_all.49
  33.8 2.5 %fusion.39 = f32[6,256,128]{2,1,0:T(8,128)} fusion(f32[6,256,128]{1,2,0:T(8,128)S(1)} %convolution_bitcast_fusion, f32[6,256,128]{1,2,0:T(8,128)S(1)} %fusion, f32[256,128]{0,1:T(8,128)S(1)} %get-tuple-element.7, f32[256,128]{0,1:T(8,128)S(1)} %get-tuple-element.8), kind=kOutput, calls=%fused_computation.70 | convolution fusion | flops 302809088 | bytes 2621440 | tf_op jit(solution)/shard_map/ckn,nm->ckm/dot_general | solution.py:62
  36.3 2.3 %all-to-all-done.2 = bf16[4,6,4096]{2,1,0:T(8,128)(2,1)} async-done(((bf16[4,6,4096]{2,1,0:T(8,128)(2,1)}), bf16[4,6,4096]{2,1,0:T(8,128)(2,1)}, u32[]{:S(2)}, u32[]{:S(2)}) %all-to-all-start.2) | async-done | bytes 196640 | tf_op jit(solution)/shard_map/all_to_all | solution.py:93
  38.6 4.4 %all-to-all-start = ((bf16[4,6,4096]{2,1,0:T(8,128)(2,1)}), bf16[4,6,4096]{2,1,0:T(8,128)(2,1)}, u32[]{:S(2)}, u32[]{:S(2)}) async-start(bf16[4,6,4096]{2,1,0:T(8,128)(2,1)} %all_to_all.49), calls=%async_computation | async-start | bytes 524288 | tf_op jit(solution)/shard_map/all_to_all | solution.py:91
  45.0 2.0 %mul.450 = f32[6,128,128]{2,1,0:T(8,128)} reshape(f32[6,4,4096]{2,1,0:T(4,128)} %copy.64) | data formatting | bytes 786432 | tf_op jit(solution)/shard_map/mul | solution.py:101
  47.1 1.8 %fusion.1 = f32[6,256,128]{1,2,0:T(8,128)S(1)} fusion(f32[6,128,128]{2,1,0:T(8,128)} %mul.450, f32[256,256]{1,0:T(8,128)} %fusion.35), kind=kOutput, calls=%fused_computation.11 | convolution fusion | flops 302186496 | bytes 1310720 | tf_op jit(solution)/shard_map/kn,cnm->ckm/dot_general | solution.py:58
  48.9 1.8 %convolution_bitcast_fusion.1 = f32[6,256,128]{1,2,0:T(8,128)S(1)} fusion(f32[6,128,128]{2,1,0:T(8,128)} %mul.450, f32[256,256]{1,0:T(8,128)} %fusion.36), kind=kOutput, calls=%fused_computation.12 | convolution fusion | flops 301989888 | bytes 1310720 | tf_op jit(solution)/shard_map/kn,cnm->ckm/dot_general | solution.py:58
  57.3 1.7 multiply_subtract_fusion
  67.0 14.9 %all_to_all.67 = bf16[6,4,4096]{2,0,1:T(8,128)(2,1)S(1)} all-to-all(bf16[6,4,4096]{2,0,1:T(8,128)(2,1)S(1)} %fusion.16), channel_id=1, replica_groups=mesh['seg'=4,'ch_0'=4,'ch_1'=4,'ch_2'=2,'ch_3'=2] {'seg'}, dimensions={1} | all-to-all | bytes 393216 | tf_op jit(solution)/shard_map/all_to_all | solution.py:113
  82.9 8.6 %all_to_all.68 = bf16[2,2,24576]{2,1,0:T(2,128)(2,1)S(1)} all-to-all(bf16[2,2,24576]{2,1,0:T(2,128)(2,1)S(1)} %reshape.92), channel_id=1, replica_groups=mesh['seg'=4,'ch_0'=4,'ch_1'=4,'ch_2'=2,'ch_3'=2] {'ch_3'}, dimensions={0} | all-to-all | bytes 393216 | tf_op jit(solution)/shard_map/all_to_all | solution.py:30
  92.1 15.8 %all_to_all.69 = bf16[32,2,1536]{2,1,0:T(2,128)(2,1)S(1)} all-to-all(bf16[32,2,1536]{2,1,0:T(2,128)(2,1)S(1)} %reshape.94), channel_id=1, replica_groups=mesh['seg'=4,'ch_0'=4,'ch_1'=4,'ch_2'=2,'ch_3'=2] {'ch_0','ch_1','ch_2'}, dimensions={0} | all-to-all | bytes 393216 | tf_op jit(solution)/shard_map/all_to_all | solution.py:30
  107.9 2.5 %stack.2 = bf16[64,24,1536]{2,1,0:T(8,128)(2,1)} broadcast(bf16[24,1536]{1,0:T(8,128)(2,1)S(1)} %copy-done.5), dimensions={1,2} | broadcast | bytes 4792320 | tf_op jit(solution)/shard_map/stack | solution.py:118
  110.4 6.6 %all-to-all-start.6 = ((bf16[64,24,1536]{2,1,0:T(8,128)(2,1)}), bf16[64,24,1536]{2,1,0:T(8,128)(2,1)}, u32[]{:S(2)}, u32[]{:S(2)}) async-start(bf16[64,24,1536]{2,1,0:T(8,128)(2,1)} %stack.2), calls=%async_computation.6 | async-start | bytes 9437184 | tf_op jit(solution)/shard_map/all_to_all | solution.py:118
  117.2 59.1 %all-to-all-done.6 = bf16[64,24,1536]{2,1,0:T(8,128)(2,1)} async-done(((bf16[64,24,1536]{2,1,0:T(8,128)(2,1)}), bf16[64,24,1536]{2,1,0:T(8,128)(2,1)}, u32[]{:S(2)}, u32[]{:S(2)}) %all-to-all-start.6) | async-done | bytes 4718624 | tf_op jit(solution)/shard_map/all_to_all | solution.py:118
  176.4 4.0 %convolution_convert_fusion = bf16[64,1536]{1,0:T(8,128)(2,1)} fusion(bf16[1536,64]{1,0:T(8,128)(2,1)S(1)} %bitcast.94, bf16[1536,1536]{1,0:T(8,128)(2,1)} %bitcast.20), kind=kOutput, calls=%fused_computation | convolution fusion | flops 302088192 | bytes 5111808 | tf_op jit(solution)/shard_map/dot_general | solution.py:115
  (43 shorter events, 20.7 us)
Async XLA Ops:
  0.0 13.1 %copy-start = (f32[24,16384]{1,0:T(8,128)S(1)}, f32[24,16384]{1,0:T(8,128)}, u32[]{:S(2)}) copy-start(f32[24,16384]{1,0:T(8,128)} %param.9) | copy-start | bytes 4718596
  1.8 21.8 %all-to-all-start.1 = ((bf16[4,6,4096]{2,1,0:T(8,128)(2,1)}), bf16[4,6,4096]{2,1,0:T(8,128)(2,1)}, u32[]{:S(2)}, u32[]{:S(2)}) async-start(bf16[4,6,4096]{2,1,0:T(8,128)(2,1)} %all_to_all.51), calls=%async_computation.1 | async-start | bytes 524288 | tf_op jit(solution)/shard_map/all_to_all | solution.py:92
  15.5 16.5 %copy-start.6 = (f32[24]{0:T(128)S(1)}, f32[24]{0:T(128)}, u32[]{:S(2)}) copy-start(f32[24]{0:T(128)} %param.10) | copy-start | bytes 292
  23.7 14.9 %all-to-all-start.2 = ((bf16[4,6,4096]{2,1,0:T(8,128)(2,1)}), bf16[4,6,4096]{2,1,0:T(8,128)(2,1)}, u32[]{:S(2)}, u32[]{:S(2)}) async-start(bf16[4,6,4096]{2,1,0:T(8,128)(2,1)} %all_to_all.53), calls=%async_computation.2 | async-start | bytes 524288 | tf_op jit(solution)/shard_map/all_to_all | solution.py:93
  38.6 27.0 %all-to-all-start = ((bf16[4,6,4096]{2,1,0:T(8,128)(2,1)}), bf16[4,6,4096]{2,1,0:T(8,128)(2,1)}, u32[]{:S(2)}, u32[]{:S(2)}) async-start(bf16[4,6,4096]{2,1,0:T(8,128)(2,1)} %all_to_all.49), calls=%async_computation | async-start | bytes 524288 | tf_op jit(solution)/shard_map/all_to_all | solution.py:91
  52.4 4.9 %copy-start.1 = (f32[6,256,128]{2,1,0:T(8,128)S(1)}, f32[6,256,128]{2,1,0:T(8,128)}, u32[]{:S(2)}) copy-start(f32[6,256,128]{2,1,0:T(8,128)} %fusion.39) | copy-start | bytes 2359300
  52.4 4.9 %copy-start.2 = (f32[6,256,128]{2,1,0:T(8,128)S(1)}, f32[6,256,128]{2,1,0:T(8,128)}, u32[]{:S(2)}) copy-start(f32[6,256,128]{2,1,0:T(8,128)} %convolution_add_fusion.2) | copy-start | bytes 2359300
  58.9 4.7 %copy-start.3 = (f32[256,256]{1,0:T(8,128)S(1)}, f32[256,256]{1,0:T(8,128)}, u32[]{:S(2)}) copy-start(f32[256,256]{1,0:T(8,128)} %fusion.36) | copy-start | bytes 786436
  60.1 4.4 %copy-start.4 = (f32[256,256]{1,0:T(8,128)S(1)}, f32[256,256]{1,0:T(8,128)}, u32[]{:S(2)}) copy-start(f32[256,256]{1,0:T(8,128)} %fusion.35) | copy-start | bytes 786436
  65.3 42.7 %copy-start.5 = (bf16[24,1536]{1,0:T(8,128)(2,1)S(1)}, bf16[24,1536]{1,0:T(8,128)(2,1)}, u32[]{:S(2)}) copy-start(bf16[24,1536]{1,0:T(8,128)(2,1)} %param.11) | copy-start | bytes 221188
  110.4 66.0 %all-to-all-start.6 = ((bf16[64,24,1536]{2,1,0:T(8,128)(2,1)}), bf16[64,24,1536]{2,1,0:T(8,128)(2,1)}, u32[]{:S(2)}, u32[]{:S(2)}) async-start(bf16[64,24,1536]{2,1,0:T(8,128)(2,1)} %stack.2), calls=%async_computation.6 | async-start | bytes 9437184 | tf_op jit(solution)/shard_map/all_to_all | solution.py:118
